TPU v7x, 32 devices: a whole 2x2x4 slice. The times are simulated.
32 devices in a mesh: gx: 2 (over x), gy: 4 (over z), gz: 4 (over y, core).
Axes of the slice: x: 2, y: 2, z: 4, core: 2. Of those that a mesh axis runs over, the one named last changes fastest.
Arguments:
- acts: bfloat16 [40960, 768], P(('gx', 'gy', 'gz')), may hold values from -6 to 6
- grads_out: bfloat16 [40960, 768], P(('gx', 'gy', 'gz')), may hold values from -0.03125 to 0.03125
- master: float32 [4608, 128], P(('gx', 'gy', 'gz')), may hold values from -0.3 to 0.3
- moment: float32 [4608, 128], P(('gx', 'gy', 'gz')), may hold values from -6 to 6
- second: float32 [4608, 128], P(('gx', 'gy', 'gz')), may hold values from 0.1 to 2
Outputs:
- master_new: float32 [4608, 128], P(('gx', 'gy', 'gz'))
- moment_new: float32 [4608, 128], P(('gx', 'gy', 'gz'))
- second_new: float32 [4608, 128], P(('gx', 'gy', 'gz'))
- weights: bfloat16 [768, 768], replicated
All inputs are finite; a program needn't handle non-finite values.
Results may differ from a plain program's by a relative error of at most 0.003.
Values may be sent and summed in bfloat16 or wider, within the bound.
A program may use at most 64 MiB of HBM per device.

v0:
```python
import jax
import jax.numpy as jnp
from jax import lax
from jax.sharding import PartitionSpec as P

STEP = 1000


def shards(acts, grads_out, master, moment, second):
    width_in = acts.shape[1]
    width_out = grads_out.shape[1]
    lane = master.shape[1]
    total_rows = width_in * width_out // lane
    local_grad = lax.dot_general(
        acts, grads_out, (((0,), (0,)), ((), ())), preferred_element_type=jnp.float32
    )
    local_flat = local_grad.reshape(total_rows, lane)
    partial_value = lax.psum_scatter(
        local_flat.astype(jnp.bfloat16), "gx", scatter_dimension=0, tiled=True
    ).astype(jnp.float32)
    partial_value = lax.psum_scatter(
        partial_value.astype(jnp.bfloat16), "gy", scatter_dimension=0, tiled=True
    ).astype(jnp.float32)
    gradient = lax.psum_scatter(
        partial_value.astype(jnp.bfloat16), "gz", scatter_dimension=0, tiled=True
    ).astype(jnp.float32)
    moment_new = 0.9 * moment + 0.1 * gradient
    second_new = 0.95 * second + 0.05 * gradient * gradient
    first_fix = 1.0 - 0.9**STEP
    second_fix = 1.0 - 0.95**STEP
    ratio = moment_new / first_fix / (jnp.sqrt(second_new / second_fix) + 1e-08)
    master_new = master - 0.01 * (ratio + 0.01 * master)
    rounded = master_new.astype(jnp.bfloat16)
    gathered = lax.all_gather(rounded, "gz", axis=0, tiled=True)
    gathered = lax.all_gather(gathered, "gy", axis=0, tiled=True)
    gathered = lax.all_gather(gathered, "gx", axis=0, tiled=True)
    weights = gathered.reshape(width_in, width_out)
    return (master_new, moment_new, second_new, weights)


def solution(mesh):
    return jax.shard_map(
        shards,
        mesh=mesh,
        in_specs=(
            P(("gx", "gy", "gz"), None),
            P(("gx", "gy", "gz"), None),
            P(("gx", "gy", "gz"), None),
            P(("gx", "gy", "gz"), None),
            P(("gx", "gy", "gz"), None),
        ),
        out_specs=(
            P(("gx", "gy", "gz"), None),
            P(("gx", "gy", "gz"), None),
            P(("gx", "gy", "gz"), None),
            P(),
        ),
        check_vma=False,
    )
```

profile of v0, /device:TPU:0, one launch (start us, length us, event | category | flops | bytes accessed | tf_op | source)
XLA Modules:
  0.0 141.0 jit_solution(13236243267090482629)
XLA Ops:
  7.2 0.0 copy-start
  7.2 0.0 reduce-scatter.4.cloned.1.call-start
  7.2 1.5 %copy-done = bf16[1280,768]{1,0:T(8,128)(2,1)S(1)} copy-done((bf16[1280,768]{1,0:T(8,128)(2,1)S(1)}, bf16[1280,768]{1,0:T(8,128)(2,1)}, u32[]{:S(2)}) %copy-start) | copy-done | bytes 1966104
  8.7 3.3 %convolution_convert_fusion = bf16[768,768]{1,0:T(8,128)(2,1)S(1)} fusion(bf16[1280,768]{1,0:T(8,128)(2,1)S(1)} %copy-done, bf16[1280,768]{1,0:T(8,128)(2,1)} %param.6), kind=kOutput, calls=%fused_computation | convolution fusion | flops 1510539264 | bytes 5111808 | tf_op jit(solution)/shard_map/dot_general | solution.py:14
  12.0 0.0 copy-start.1
  12.0 0.0 copy-start.2
  12.0 0.0 copy-start.3
  12.1 1.9 %convert_element_type.17 = bf16[4608,128]{1,0:T(8,128)(2,1)} reshape(bf16[768,768]{1,0:T(8,128)(2,1)S(1)} %convolution_convert_fusion) | data formatting | bytes 2359296 | tf_op jit(solution)/shard_map/convert_element_type | solution.py:19
  13.9 0.0 reduce-scatter.4.cloned.1.call-update
  13.9 0.0 reduce-scatter.6.cloned.1.call-start
  14.0 24.7 %reduce-scatter.4.cloned.1.call-done = bf16[2304,128]{1,0:T(8,128)(2,1)} async-done(((bf16[4608,128]{1,0:T(8,128)(2,1)}), bf16[2304,128]{1,0:T(8,128)(2,1)}) %reduce-scatter.4.cloned.1.call-update) | async-done | bytes 589840 | tf_op jit(solution)/shard_map/reduce_scatter | solution.py:18
  38.7 0.0 reduce-scatter.6.cloned.1.call-update
  38.7 0.0 reduce-scatter.8.cloned.1.call-start
  38.7 24.4 %reduce-scatter.6.cloned.1.call-done = bf16[576,128]{1,0:T(8,128)(2,1)} async-done(((bf16[2304,128]{1,0:T(8,128)(2,1)}), bf16[576,128]{1,0:T(8,128)(2,1)}) %reduce-scatter.6.cloned.1.call-update) | async-done | bytes 147472 | tf_op jit(solution)/shard_map/reduce_scatter | solution.py:21
  63.1 0.0 reduce-scatter.8.cloned.1.call-update
  63.1 0.0 all-gather.2.cloned.1.call-start
  63.2 20.5 %reduce-scatter.8.cloned.1.call-done = bf16[144,128]{1,0:T(8,128)(2,1)} async-done(((bf16[576,128]{1,0:T(8,128)(2,1)}), bf16[144,128]{1,0:T(8,128)(2,1)}) %reduce-scatter.8.cloned.1.call-update) | async-done | bytes 36880 | tf_op jit(solution)/shard_map/reduce_scatter | solution.py:24
  83.7 0.0 copy-done.1
  83.7 0.0 copy-done.2
  83.7 0.0 copy-done.3
  83.7 1.5 %fusion.2 = (bf16[144,128]{1,0:T(8,128)(2,1)S(1)}, f32[144,128]{1,0:T(8,128)}, f32[144,128]{1,0:T(8,128)}, f32[144,128]{1,0:T(8,128)}) fusion(f32[144,128]{1,0:T(8,128)S(1)} %copy-done.1, bf16[144,128]{1,0:T(8,128)(2,1)} %reduce-scatter.8.cloned.1.call-done, f32[144,128]{1,0:T(8,128)S(1)} %copy-done.2, f32[144,128]{1,0:T(8,128)S(1)} %copy-done.3), kind=kLoop, calls=%fused_computation.6 | loop fusion | flops 276480 | bytes 516096 | tf_op jit(solution)/shard_map/convert_element_type | solution.py:33
  85.2 5.4 %all_gather.9 = bf16[576,128]{1,0:T(8,128)(2,1)S(1)} all-gather(bf16[144,128]{1,0:T(8,128)(2,1)S(1)} %get-tuple-element.4), channel_id=1, replica_groups=mesh['gx'=2,'gy'=4,'gz'=4] {'gz'}, dimensions={0}, use_global_device_ids=true | all-gather | bytes 184320 | tf_op jit(solution)/shard_map/all_gather | solution.py:34
  90.6 17.2 %all_gather.10 = bf16[2304,128]{1,0:T(8,128)(2,1)} all-gather(bf16[576,128]{1,0:T(8,128)(2,1)S(1)} %all_gather.9), channel_id=1, replica_groups=mesh['gx'=2,'gy'=4,'gz'=4] {'gy'}, dimensions={0}, use_global_device_ids=true | all-gather | bytes 737280 | tf_op jit(solution)/shard_map/all_gather | solution.py:35
  107.8 0.0 all-gather.2.cloned.1.call-update
  107.8 23.3 %all-gather.2.cloned.1.call-done = bf16[4608,128]{1,0:T(8,128)(2,1)} async-done(((bf16[2304,128]{1,0:T(8,128)(2,1)}), bf16[4608,128]{1,0:T(8,128)(2,1)}) %all-gather.2.cloned.1.call-update) | async-done | bytes 1179664 | tf_op jit(solution)/shard_map/all_gather | solution.py:36
  131.1 3.3 %reshape.13 = bf16[768,768]{1,0:T(8,128)(2,1)} reshape(bf16[4608,128]{1,0:T(8,128)(2,1)} %all-gather.2.cloned.1.call-done) | data formatting | bytes 2359296 | tf_op jit(solution)/shard_map/reshape | solution.py:37
Async XLA Ops:
  7.2 1.6 %copy-start = (bf16[1280,768]{1,0:T(8,128)(2,1)S(1)}, bf16[1280,768]{1,0:T(8,128)(2,1)}, u32[]{:S(2)}) copy-start(bf16[1280,768]{1,0:T(8,128)(2,1)} %param.5) | copy-start | bytes 5898244
  7.2 31.5 %reduce-scatter.4.cloned.1.call-start = ((), (), s32[]{:S(2)}) async-start(), calls=%async_computation.3 | async-start | bytes 1769472 | tf_op jit(solution)/shard_map/reduce_scatter | solution.py:18
  12.0 71.7 %copy-start.1 = (f32[144,128]{1,0:T(8,128)S(1)}, f32[144,128]{1,0:T(8,128)}, u32[]{:S(2)}) copy-start(f32[144,128]{1,0:T(8,128)} %param.7) | copy-start | bytes 221188
  12.0 71.7 %copy-start.2 = (f32[144,128]{1,0:T(8,128)S(1)}, f32[144,128]{1,0:T(8,128)}, u32[]{:S(2)}) copy-start(f32[144,128]{1,0:T(8,128)} %param.9) | copy-start | bytes 221188
  12.0 71.7 %copy-start.3 = (f32[144,128]{1,0:T(8,128)S(1)}, f32[144,128]{1,0:T(8,128)}, u32[]{:S(2)}) copy-start(f32[144,128]{1,0:T(8,128)} %param.8) | copy-start | bytes 221188
  13.9 49.2 %reduce-scatter.6.cloned.1.call-start = ((), (), s32[]{:S(2)}) async-start(), calls=%async_computation.4 | async-start | bytes 737280 | tf_op jit(solution)/shard_map/reduce_scatter | solution.py:21
  38.7 45.0 %reduce-scatter.8.cloned.1.call-start = ((), (), s32[]{:S(2)}) async-start(), calls=%async_computation.5 | async-start | bytes 184320 | tf_op jit(solution)/shard_map/reduce_scatter | solution.py:24
  63.1 68.0 %all-gather.2.cloned.1.call-start = ((), (), s32[]{:S(2)}) async-start(), calls=%async_computation.6 | async-start | bytes 1769472 | tf_op jit(solution)/shard_map/all_gather | solution.py:36
Sparse Core Ops, SparseCore 0:
  14.1 24.5 reduce-scatter.3
  40.9 22.1 reduce-scatter.5
  65.5 18.1 reduce-scatter.7
  108.0 23.0 all-gather.1
where the time goes:
time: 141 us
  waiting for transfers between devices  92.9 us (66%)
  blocking collectives  22.6 us (16%)
  between operations  13.8 us (10%)
  local copies, waits for them, and re-layouts  6.73 us (5%)
  matrix products  3.29 us (2%)
  other arithmetic  1.48 us (1%)
    reduce_scatter x1, waiting for transfers between devices, shards(): lax.psum_scatter(local_flat.astype(jnp.bfloat16), 'gx', scatter_dimension...  24.7 us
    reduce_scatter x1, waiting for transfers between devices, shards(): lax.psum_scatter(partial_value.astype(jnp.bfloat16), 'gy', scatter_dimens...  24.4 us
    all_gather x1, waiting for transfers between devices, shards(): gathered = lax.all_gather(gathered, 'gx', axis=0, tiled=True)  23.3 us
    reduce_scatter x1, waiting for transfers between devices, shards(): lax.psum_scatter(partial_value.astype(jnp.bfloat16), 'gz', scatter_dimens...  20.5 us
    all_gather x1, blocking collectives, shards(): gathered = lax.all_gather(gathered, 'gy', axis=0, tiled=True)  17.2 us
    all_gather x1, blocking collectives, shards(): gathered = lax.all_gather(rounded, 'gz', axis=0, tiled=True)  5.45 us
    reshape x1, local copies, waits for them, and re-layouts, shards(): weights = gathered.reshape(width_in, width_out)  3.35 us
    dot_general x1, matrix products, shards(): lax.dot_general(acts, grads_out, (((0,), (0,)), ((), ())), preferred_elem...  3.29 us
  transfers between devices with their start and end apart: 4, of which 4 were waited for; matrix products, arithmetic and copies ran while one was open for 0% of the time, Pallas kernels for 0%

commit v1 on v0

v1 whole, which is shorter than its diff:
```python
import functools
import itertools

import jax
import jax.numpy as jnp
from jax import lax
from jax.experimental import pallas as pl
from jax.experimental.pallas import tpu as pltpu
from jax.sharding import PartitionSpec as P

STEP = 1000
MESH = pl.DeviceIdType.MESH
CORES = 2


def adam(gradient, master, moment, second):
    moment_new = 0.9 * moment + 0.1 * gradient
    second_new = 0.95 * second + 0.05 * gradient * gradient
    first_fix = 1.0 - 0.9**STEP
    second_fix = 1.0 - 0.95**STEP
    ratio = moment_new / first_fix / (jnp.sqrt(second_new / second_fix) + 1e-08)
    master_new = master - 0.01 * (ratio + 0.01 * master)
    return master_new, moment_new, second_new


def shards(acts, grads_out, master, moment, second):
    width_in = acts.shape[1]
    width_out = grads_out.shape[1]
    lane = master.shape[1]
    total_rows = width_in * width_out // lane
    local_grad = lax.dot_general(
        acts, grads_out, (((0,), (0,)), ((), ())), preferred_element_type=jnp.float32
    )
    value = local_grad.reshape(total_rows, lane)
    for axis in ("gx", "gy", "gz"):
        value = lax.psum_scatter(
            value.astype(jnp.bfloat16), axis, scatter_dimension=0, tiled=True
        ).astype(jnp.float32)
    master_new, moment_new, second_new = adam(value, master, moment, second)
    gathered = master_new.astype(jnp.bfloat16)
    for axis in ("gz", "gy", "gx"):
        gathered = lax.all_gather(gathered, axis, axis=0, tiled=True)
    weights = gathered.reshape(width_in, width_out)
    return (master_new, moment_new, second_new, weights)


def flip(value, bits):
    bit = 1
    while bit <= bits:
        if bits & bit:
            value = value + bit - 2 * bit * (lax.rem(value // bit, 2))
        bit *= 2
    return value


def kernel(
    nx, nz, ny,
    acts_ref, grads_ref, master_ref, moment_ref, second_ref,
    master_out, moment_out, second_out, weights_out,
    part, pair_out, pair_in, out, inn, full,
    pair_send, pair_recv, link_send, link_recv,
    gather_send, gather_recv, twin_send, twin_recv,
):
    x = lax.axis_index("gx")
    z = lax.axis_index("gy")
    g = lax.axis_index("gz")
    y = g // CORES
    core = lax.rem(g, CORES)
    lane = master_ref.shape[1]
    rows = acts_ref.shape[1] // (nx * nz * ny * CORES)
    strips = grads_ref.shape[1] // lane
    block_rows = rows * strips

    def peer(kx=0, kz=0, ky=0, kc=0):
        return (flip(x, kx), flip(z, kz), flip(y, ky) * CORES + flip(core, kc))

    def owner(kx, kz, ky, kc):
        px, pz, pg = peer(kx, kz, ky, kc)
        return (px * nz + pz) * (ny * CORES) + pg

    def slot(kx, kz, ky):
        return (kx * nz + kz) * ny + ky

    xs, zs, ys = range(1, nx), range(1, nz), range(1, ny)
    peers = [peer(kc=1)] + [peer(kx=k) for k in xs]
    peers += [peer(ky=k) for k in ys] + [peer(kz=k) for k in zs]

    barrier = pltpu.get_barrier_semaphore()
    for target in peers:
        pl.semaphore_signal(barrier, inc=1, device_id=target, device_id_type=MESH)

    part[...] = lax.dot_general(
        acts_ref[...], grads_ref[...], (((0,), (0,)), ((), ())),
        preferred_element_type=jnp.float32,
    )

    def mine(kx, kz, ky, kc):
        top = pl.multiple_of(owner(kx, kz, ky, kc) * rows, 8)
        return jnp.concatenate(
            [part[pl.ds(top, rows), s * lane:(s + 1) * lane] for s in range(strips)], axis=0
        )

    def x_first(kz):
        return kz % 2 == 0

    first, second_step, third = [], [], []
    for kz in reversed(range(nz)):
        for ky, kx in itertools.product(reversed(range(ny)), reversed(range(nx))):
            if (kx if x_first(kz) else ky) != 0:
                first.append((kx, kz, ky))
            elif (ky if x_first(kz) else kx) != 0:
                second_step.append((kx, kz, ky))
            else:
                third.append((kx, kz, ky))
    first.sort(key=lambda k: -(k[0] != 0) - (k[2] != 0))

    pl.semaphore_wait(barrier, len(peers))

    started = []

    def send(src, dst, send_sem, recv_sem, target):
        copy = pltpu.make_async_remote_copy(
            src_ref=src, dst_ref=dst, send_sem=send_sem, recv_sem=recv_sem,
            device_id=target, device_id_type=MESH,
        )
        copy.start()
        started.append(copy)

    def arrived(dst, send_sem, recv_sem):
        pltpu.make_async_remote_copy(
            src_ref=dst, dst_ref=dst, send_sem=send_sem, recv_sem=recv_sem,
            device_id=peer(kc=1), device_id_type=MESH,
        ).wait_recv()

    for k in first + second_step + third:
        i = slot(*k)
        pair_out[i] = mine(*k, 1).astype(jnp.bfloat16)
        send(pair_out.at[i], pair_in.at[i], pair_send.at[i], pair_recv.at[i], peer(kc=1))

    def take(i):
        arrived(inn.at[i], link_send.at[i], link_recv.at[i])
        return inn[i].astype(jnp.float32)

    def total(k):
        kx, kz, ky = k
        i = slot(*k)
        arrived(pair_in.at[i], pair_send.at[i], pair_recv.at[i])
        value = mine(*k, 0) + pair_in[i].astype(jnp.float32)
        if x_first(kz):
            if kx == 0:
                for p in xs:
                    value += take(slot(p, kz, ky))
                if ky == 0:
                    for p in ys:
                        value += take(slot(0, kz, p))
        else:
            if ky == 0:
                for p in ys:
                    value += take(slot(kx, kz, p))
                if kx == 0:
                    for p in xs:
                        value += take(slot(p, kz, 0))
        return value

    def pass_on(k, target):
        i = slot(*k)
        out[i] = total(k).astype(jnp.bfloat16)
        send(out.at[i], inn.at[i], link_send.at[i], link_recv.at[i], target)

    for k in first:
        kx, kz, ky = k
        pass_on(k, peer(kx=kx) if x_first(kz) else peer(ky=ky))
    for k in second_step:
        kx, kz, ky = k
        pass_on(k, peer(ky=ky) if x_first(kz) else peer(kx=kx))
    gradient = None
    for k in third:
        if k[1] != 0:
            pass_on(k, peer(kz=k[1]))
        else:
            gradient = total(k)
    for kz in zs:
        gradient += take(slot(0, kz, 0))

    me = owner(0, 0, 0, 0)
    updated = []
    for s in range(strips):
        at = pl.ds(s, rows, stride=strips)
        master_new, moment_new, second_new = adam(
            gradient[s * rows:(s + 1) * rows],
            master_ref[at, :], moment_ref[at, :], second_ref[at, :],
        )
        master_out[at, :] = master_new
        moment_out[at, :] = moment_new
        second_out[at, :] = second_new
        updated.append(master_new)
    full[me] = jnp.concatenate(updated, axis=0).astype(jnp.bfloat16)

    def forward(k, kx, kz, ky):
        i = slot(kx, kz, ky)
        here = full.at[owner(*k, 0)]
        target = peer(kx=kx ^ k[0], kz=kz ^ k[1], ky=ky ^ k[2])
        send(here, here, gather_send.at[i], gather_recv.at[i], target)

    def twin(k):
        i = slot(*k)
        here = full.at[owner(*k, 0)]
        send(here, here, twin_send.at[i], twin_recv.at[i], peer(kc=1))

    def receive(k):
        i = slot(*k)
        arrived(full.at[owner(*k, 0)], gather_send.at[i], gather_recv.at[i])

    def spread(k):
        kx, kz, ky = k
        if kx == 0 and ky == 0 and kz == 0:
            for p in reversed(zs):
                forward(k, 0, p, 0)
        if x_first(kz):
            if kx == 0 and ky == 0:
                for p in ys:
                    forward(k, 0, kz, p)
            if kx == 0:
                for p in xs:
                    forward(k, p, kz, ky)
        else:
            if kx == 0 and ky == 0:
                for p in xs:
                    forward(k, p, kz, 0)
            if ky == 0:
                for p in ys:
                    forward(k, kx, kz, p)
        twin(k)

    def middle(kz):
        if x_first(kz):
            return [(0, kz, p) for p in ys]
        return [(p, kz, 0) for p in xs]

    def last(kz):
        if x_first(kz):
            return [(p, kz, q) for q in range(ny) for p in xs]
        return [(p, kz, q) for p in range(nx) for q in ys]

    order = [(0, 0, 0)] + middle(0)
    for kz in zs:
        order += [(0, kz, 0)] + (last(kz - 1) if kz == 1 else middle(kz - 1))
    order += middle(nz - 1)
    for kz in zs:
        order += last(kz)
    seen = []
    for k in order:
        if k in seen:
            continue
        seen.append(k)
        if k != (0, 0, 0):
            receive(k)
        spread(k)

    chip_rows = CORES * rows
    for k in seen:
        i = slot(*k)
        arrived(full.at[owner(*k, 1)], twin_send.at[i], twin_recv.at[i])
        pair = owner(*k, 0) // CORES
        top = pl.multiple_of(pair * chip_rows, 16)
        low = full[pair * CORES].astype(jnp.float32)
        high = full[pair * CORES + 1].astype(jnp.float32)
        for s in range(strips):
            both = jnp.concatenate(
                [low[s * rows:(s + 1) * rows], high[s * rows:(s + 1) * rows]], axis=0
            )
            weights_out[pl.ds(top, chip_rows), s * lane:(s + 1) * lane] = both.astype(jnp.bfloat16)

    for copy in started:
        copy.wait_send()


def fused(nx, nz, ny, acts, grads_out, master, moment, second):
    width_in, width_out = acts.shape[1], grads_out.shape[1]
    flat, lane = master.shape
    chips = nx * nz * ny
    block = (flat, lane)
    vmem = pl.BlockSpec(memory_space=pltpu.VMEM)
    sems = pltpu.SemaphoreType.DMA((chips,))
    return pl.pallas_call(
        functools.partial(kernel, nx, nz, ny),
        out_shape=(
            jax.ShapeDtypeStruct(block, jnp.float32),
            jax.ShapeDtypeStruct(block, jnp.float32),
            jax.ShapeDtypeStruct(block, jnp.float32),
            jax.ShapeDtypeStruct((width_in, width_out), jnp.bfloat16),
        ),
        in_specs=[vmem] * 5,
        out_specs=(vmem,) * 4,
        scratch_shapes=[
            pltpu.VMEM((width_in, width_out), jnp.float32),
            pltpu.VMEM((chips,) + block, jnp.bfloat16),
            pltpu.VMEM((chips,) + block, jnp.bfloat16),
            pltpu.VMEM((chips,) + block, jnp.bfloat16),
            pltpu.VMEM((chips,) + block, jnp.bfloat16),
            pltpu.VMEM((chips * CORES,) + block, jnp.bfloat16),
        ] + [sems] * 8,
        compiler_params=pltpu.CompilerParams(collective_id=0, has_side_effects=True),
    )(acts, grads_out, master, moment, second)


def power_of_two(n):
    return n & (n - 1) == 0


def body(mesh, acts, grads_out, master, moment, second):
    nx, nz, ng = mesh.shape["gx"], mesh.shape["gy"], mesh.shape["gz"]
    devices = nx * nz * ng
    whole_rows = acts.shape[1] % (8 * devices) == 0 and grads_out.shape[1] % master.shape[1] == 0
    even = (grads_out.shape[1] // master.shape[1]) % 2 == 0
    if whole_rows and even and ng % CORES == 0 and all(map(power_of_two, (nx, nz, ng))):
        return fused(nx, nz, ng // CORES, acts, grads_out, master, moment, second)
    return shards(acts, grads_out, master, moment, second)


def solution(mesh):
    split = P(("gx", "gy", "gz"), None)
    return jax.shard_map(
        functools.partial(body, mesh),
        mesh=mesh,
        in_specs=(split,) * 5,
        out_specs=(split, split, split, P()),
        check_vma=False,
    )
```

time: 141 us -> 43.2 us (0.31)
  waiting for transfers between devices: 92.9 us -> 0 us
  Pallas kernels: 0 us -> 35.3 us
  blocking collectives: 22.6 us -> 0 us
  between operations: 13.8 us -> 0.64 us
  matrix products: 3.29 us -> 0 us
  other arithmetic: 1.48 us -> 0 us
    reduce_scatter x3 -> x0, waiting for transfers between devices: 69.6 us -> none  [the longest x1 24.7 us: shards(): lax.psum_scatter(local_flat.astype(jnp.bfloat16), 'gx', scatter_dimension...]
    pallas_call x0 -> x1, Pallas kernels: none -> 35.3 us  [fused(): pl.pallas_call(functools.partial(kernel, nx, nz, ny), out_shape=(jax.Shap...]
    all_gather x1 -> x0, waiting for transfers between devices: 23.3 us -> none  [shards(): gathered = lax.all_gather(gathered, 'gx', axis=0, tiled=True)]
    all_gather x2 -> x0, blocking collectives: 22.6 us -> none  [the longest x1 17.2 us: shards(): gathered = lax.all_gather(gathered, 'gy', axis=0, tiled=True)]
    unnamed x8 -> x4, local copies, waits for them, and re-layouts: 1.52 us -> 6.92 us
    reshape x1 -> x0, local copies, waits for them, and re-layouts: 3.35 us -> none  [shards(): weights = gathered.reshape(width_in, width_out)]
    dot_general x1 -> x0, matrix products: 3.29 us -> none  [shards(): lax.dot_general(acts, grads_out, (((0,), (0,)), ((), ())), preferred_elem...]
    convert_element_type x1 -> x0, local copies, waits for them, and re-layouts: 1.87 us -> none  [shards(): local_flat.astype(jnp.bfloat16)]
  transfers between devices with their start and end apart: 4 -> 0, of which waited for: 4 -> 0; matrix products, arithmetic and copies ran while one was open for 0% -> 0% of each run, Pallas kernels for 0% -> 0%
where the time goes in v1:
time: 43.2 us; the launch traced here: 42.9 us
  Pallas kernels  35.3 us (82%)
  local copies, waits for them, and re-layouts  6.92 us (16%)
  between operations  0.64 us (1%)
    pallas_call x1, Pallas kernels, fused(): pl.pallas_call(functools.partial(kernel, nx, nz, ny), out_shape=(jax.Shap...  35.3 us
    unnamed x4, local copies, waits for them, and re-layouts  6.92 us

profile of v1, /device:TPU:0, one launch (start us, length us, event | category | flops | bytes accessed | tf_op | source)
XLA Modules:
  0.0 42.9 jit_solution(13873366237263694697)
XLA Ops:
  0.6 35.3 %shard_map.84 = (f32[144,128]{1,0:T(8,128)}, f32[144,128]{1,0:T(8,128)}, f32[144,128]{1,0:T(8,128)}, bf16[768,768]{1,0:T(8,128)(2,1)}) custom-call(bf16[1280,768]{1,0:T(8,128)(2,1)} %acts_ref.1, bf16[1280,768]{1,0:T(8,128)(2,1)} %grads_ref.1, f32[144,128]{1,0:T(8,128)} %master_ref.1, f32[144,128]{1,0:T(8,128)} %moment_ref.1, f32[144,128]{1,0:T(8,128)} %second_ref.1), custom_call_target="tpu_custom_call" | custom-call | tf_op jit(solution)/shard_map/pallas_call | solution.py:285
  36.0 1.5 %copy.13 = f32[144,128]{1,0:T(8,128)} copy(f32[144,128]{1,0:T(8,128)} %get-tuple-element.8) | data formatting | bytes 147456
  37.5 1.5 %copy.14 = f32[144,128]{1,0:T(8,128)} copy(f32[144,128]{1,0:T(8,128)} %get-tuple-element.9) | data formatting | bytes 147456
  39.0 1.5 %copy.15 = f32[144,128]{1,0:T(8,128)} copy(f32[144,128]{1,0:T(8,128)} %get-tuple-element.10) | data formatting | bytes 147456
  40.5 2.4 %copy.16 = bf16[768,768]{1,0:T(8,128)(2,1)} copy(bf16[768,768]{1,0:T(8,128)(2,1)} %get-tuple-element.11) | data formatting | bytes 2359296

commit v2 on v1

--- a/solution.py
+++ b/solution.py
@@ -55,10 +55,10 @@
 
 def kernel(
     nx, nz, ny,
-    acts_ref, grads_ref, master_ref, moment_ref, second_ref,
-    master_out, moment_out, second_out, weights_out,
-    part, pair_out, pair_in, out, inn, full,
-    pair_send, pair_recv, link_send, link_recv,
+    acts_ref, grads_ref, master_hbm, moment_hbm, second_hbm,
+    master_out, moment_out, second_out, full,
+    acts_in, grads_in, master_ref, moment_ref, second_ref, part, pair_out, pair_in, out, inn,
+    load, pair_send, pair_recv, link_send, link_recv,
     gather_send, gather_recv, twin_send, twin_recv,
 ):
     x = lax.axis_index("gx")
@@ -89,10 +89,21 @@
     for target in peers:
         pl.semaphore_signal(barrier, inc=1, device_id=target, device_id_type=MESH)
 
-    part[...] = lax.dot_general(
-        acts_ref[...], grads_ref[...], (((0,), (0,)), ((), ())),
-        preferred_element_type=jnp.float32,
-    )
+    width = acts_ref.shape[1] // nx
+
+    def columns(kx):
+        return pl.ds(pl.multiple_of(flip(x, kx) * width, lane), width)
+
+    loads = [pltpu.make_async_copy(grads_ref, grads_in, load.at[nx])]
+    for kx in reversed(range(nx)):
+        loads.append(
+            pltpu.make_async_copy(acts_ref.at[:, columns(kx)], acts_in.at[kx], load.at[kx])
+        )
+    state = ((master_hbm, master_ref), (moment_hbm, moment_ref), (second_hbm, second_ref))
+    for i, (src, dst) in enumerate(state):
+        loads.append(pltpu.make_async_copy(src, dst, load.at[nx + 1 + i]))
+    for copy in loads:
+        copy.start()
 
     def mine(kx, kz, ky, kc):
         top = pl.multiple_of(owner(kx, kz, ky, kc) * rows, 8)
@@ -114,8 +125,6 @@
                 third.append((kx, kz, ky))
     first.sort(key=lambda k: -(k[0] != 0) - (k[2] != 0))
 
-    pl.semaphore_wait(barrier, len(peers))
-
     started = []
 
     def send(src, dst, send_sem, recv_sem, target):
@@ -132,10 +141,20 @@
             device_id=peer(kc=1), device_id_type=MESH,
         ).wait_recv()
 
-    for k in first + second_step + third:
-        i = slot(*k)
-        pair_out[i] = mine(*k, 1).astype(jnp.bfloat16)
-        send(pair_out.at[i], pair_in.at[i], pair_send.at[i], pair_recv.at[i], peer(kc=1))
+    loads[0].wait()
+    for kx in reversed(range(nx)):
+        loads[nx - kx].wait()
+        part[columns(kx), :] = lax.dot_general(
+            acts_in[kx], grads_in[...], (((0,), (0,)), ((), ())),
+            preferred_element_type=jnp.float32,
+        )
+        if kx == nx - 1:
+            pl.semaphore_wait(barrier, len(peers))
+        for k in first + second_step + third:
+            if k[0] == kx:
+                i = slot(*k)
+                pair_out[i] = mine(*k, 1).astype(jnp.bfloat16)
+                send(pair_out.at[i], pair_in.at[i], pair_send.at[i], pair_recv.at[i], peer(kc=1))
 
     def take(i):
         arrived(inn.at[i], link_send.at[i], link_recv.at[i])
@@ -182,6 +201,8 @@
     for kz in zs:
         gradient += take(slot(0, kz, 0))
 
+    for copy in loads[nx + 1:]:
+        copy.wait()
     me = owner(0, 0, 0, 0)
     updated = []
     for s in range(strips):
@@ -257,51 +278,107 @@
             receive(k)
         spread(k)
 
-    chip_rows = CORES * rows
     for k in seen:
         i = slot(*k)
         arrived(full.at[owner(*k, 1)], twin_send.at[i], twin_recv.at[i])
-        pair = owner(*k, 0) // CORES
-        top = pl.multiple_of(pair * chip_rows, 16)
-        low = full[pair * CORES].astype(jnp.float32)
-        high = full[pair * CORES + 1].astype(jnp.float32)
-        for s in range(strips):
-            both = jnp.concatenate(
-                [low[s * rows:(s + 1) * rows], high[s * rows:(s + 1) * rows]], axis=0
-            )
-            weights_out[pl.ds(top, chip_rows), s * lane:(s + 1) * lane] = both.astype(jnp.bfloat16)
 
     for copy in started:
         copy.wait_send()
 
 
+def finish(
+    master_ref, moment_ref, second_ref, full,
+    master_out, moment_out, second_out, weights_out,
+    weights, store,
+):
+    blocks, _, lane = full.shape
+    rows = weights.shape[0] // blocks
+    strips = weights.shape[1] // lane
+    pairs = blocks // CORES
+    copies = []
+    plain = ((master_ref, master_out), (moment_ref, moment_out), (second_ref, second_out))
+    for i, (src, dst) in enumerate(plain):
+        copies.append(pltpu.make_async_copy(src, dst, store.at[i]))
+        copies[-1].start()
+    groups = 4 if pairs % 4 == 0 else 1
+    chip_rows = CORES * rows
+    for group in range(groups):
+        for pair in range(group * pairs // groups, (group + 1) * pairs // groups):
+            low = full[pair * CORES].astype(jnp.float32)
+            high = full[pair * CORES + 1].astype(jnp.float32)
+            for s in range(strips):
+                both = jnp.concatenate(
+                    [low[s * rows:(s + 1) * rows], high[s * rows:(s + 1) * rows]], axis=0
+                )
+                weights[pair * chip_rows:(pair + 1) * chip_rows, s * lane:(s + 1) * lane] = (
+                    both.astype(jnp.bfloat16)
+                )
+        span = pl.ds(group * (weights.shape[0] // groups), weights.shape[0] // groups)
+        copies.append(
+            pltpu.make_async_copy(weights.at[span, :], weights_out.at[span, :], store.at[3 + group])
+        )
+        copies[-1].start()
+    for copy in copies:
+        copy.wait()
+
+
+VMEM_BYTES = 67_043_328
+LIMIT = 24 * 1024 * 1024
+
+
 def fused(nx, nz, ny, acts, grads_out, master, moment, second):
-    width_in, width_out = acts.shape[1], grads_out.shape[1]
-    flat, lane = master.shape
+    tokens, width_in = acts.shape
+    width_out = grads_out.shape[1]
+    block = master.shape
     chips = nx * nz * ny
-    block = (flat, lane)
     vmem = pl.BlockSpec(memory_space=pltpu.VMEM)
+    hbm = pl.BlockSpec(memory_space=pl.ANY)
     sems = pltpu.SemaphoreType.DMA((chips,))
+    kept = 2 * width_in * width_out + 3 * 4 * master.size
+    limit = (VMEM_BYTES - kept - 32 * 1024) // 1024 * 1024
+    results = pl.pallas_call(
+        functools.partial(kernel, nx, nz, ny),
+        out_shape=(
+            pltpu.VMEM(block, jnp.float32),
+            pltpu.VMEM(block, jnp.float32),
+            pltpu.VMEM(block, jnp.float32),
+            pltpu.VMEM((chips * CORES,) + block, jnp.bfloat16),
+        ),
+        in_specs=[pl.BlockSpec(memory_space=pltpu.HBM)] * 5,
+        out_specs=(vmem,) * 4,
+        scratch_shapes=[
+            pltpu.VMEM((nx, tokens, width_in // nx), jnp.bfloat16),
+            pltpu.VMEM((tokens, width_out), jnp.bfloat16),
+            pltpu.VMEM(block, jnp.float32),
+            pltpu.VMEM(block, jnp.float32),
+            pltpu.VMEM(block, jnp.float32),
+            pltpu.VMEM((width_in, width_out), jnp.float32),
+            pltpu.VMEM((chips,) + block, jnp.bfloat16),
+            pltpu.VMEM((chips,) + block, jnp.bfloat16),
+            pltpu.VMEM((chips,) + block, jnp.bfloat16),
+            pltpu.VMEM((chips,) + block, jnp.bfloat16),
+            pltpu.SemaphoreType.DMA((nx + 4,)),
+        ] + [sems] * 8,
+        compiler_params=pltpu.CompilerParams(
+            collective_id=0, has_side_effects=True, vmem_limit_bytes=limit
+        ),
+    )(acts, grads_out, master, moment, second)
     return pl.pallas_call(
-        functools.partial(kernel, nx, nz, ny),
+        finish,
         out_shape=(
             jax.ShapeDtypeStruct(block, jnp.float32),
             jax.ShapeDtypeStruct(block, jnp.float32),
             jax.ShapeDtypeStruct(block, jnp.float32),
             jax.ShapeDtypeStruct((width_in, width_out), jnp.bfloat16),
         ),
-        in_specs=[vmem] * 5,
-        out_specs=(vmem,) * 4,
+        in_specs=[vmem] * 4,
+        out_specs=(hbm,) * 4,
         scratch_shapes=[
-            pltpu.VMEM((width_in, width_out), jnp.float32),
-            pltpu.VMEM((chips,) + block, jnp.bfloat16),
-            pltpu.VMEM((chips,) + block, jnp.bfloat16),
-            pltpu.VMEM((chips,) + block, jnp.bfloat16),
-            pltpu.VMEM((chips,) + block, jnp.bfloat16),
-            pltpu.VMEM((chips * CORES,) + block, jnp.bfloat16),
-        ] + [sems] * 8,
-        compiler_params=pltpu.CompilerParams(collective_id=0, has_side_effects=True),
-    )(acts, grads_out, master, moment, second)
+            pltpu.VMEM((width_in, width_out), jnp.bfloat16),
+            pltpu.SemaphoreType.DMA((7,)),
+        ],
+        compiler_params=pltpu.CompilerParams(vmem_limit_bytes=LIMIT),
+    )(*results)
 
 
 def power_of_two(n):
@@ -312,6 +389,7 @@
     nx, nz, ng = mesh.shape["gx"], mesh.shape["gy"], mesh.shape["gz"]
     devices = nx * nz * ng
     whole_rows = acts.shape[1] % (8 * devices) == 0 and grads_out.shape[1] % master.shape[1] == 0
+    whole_rows = whole_rows and acts.shape[1] % (nx * master.shape[1]) == 0
     even = (grads_out.shape[1] // master.shape[1]) % 2 == 0
     if whole_rows and even and ng % CORES == 0 and all(map(power_of_two, (nx, nz, ng))):
         return fused(nx, nz, ng // CORES, acts, grads_out, master, moment, second)

time: 43.2 us -> 34.9 us (0.81)
  local copies, waits for them, and re-layouts: 6.92 us -> 0 us
  Pallas kernels: 35.3 us -> 34 us
    unnamed x4 -> x0, local copies, waits for them, and re-layouts: 6.92 us -> none
    pallas_call x1 -> x2, Pallas kernels: 35.3 us -> 34 us  [the longest x1 32.9 us: fused(): pl.pallas_call(functools.partial(kernel, nx, nz, ny), out_shape=(pltpu.VM...]
where the time goes in v2:
time: 34.9 us; the launch traced here: 34.7 us
  Pallas kernels  34 us (97%)
  between operations  0.64 us (2%)
    pallas_call x1, Pallas kernels, fused(): pl.pallas_call(functools.partial(kernel, nx, nz, ny), out_shape=(pltpu.VM...  32.9 us
    pallas_call x1, Pallas kernels, fused(): pl.pallas_call(finish, out_shape=(jax.ShapeDtypeStruct(block, jnp.float32...  1.14 us

profile of v2, /device:TPU:0, one launch (start us, length us, event | category | flops | bytes accessed | tf_op | source)
XLA Modules:
  0.0 34.7 jit_solution(17866934021310545250)
XLA Ops:
  0.6 32.9 %shard_map.84 = (f32[144,128]{1,0:T(8,128)S(1)}, f32[144,128]{1,0:T(8,128)S(1)}, f32[144,128]{1,0:T(8,128)S(1)}, bf16[32,144,128]{2,1,0:T(8,128)(2,1)S(1)}) custom-call(bf16[1280,768]{1,0:T(8,128)(2,1)} %acts_ref.1, bf16[1280,768]{1,0:T(8,128)(2,1)} %grads_ref.1, f32[144,128]{1,0:T(8,128)} %master_hbm.1, f32[144,128]{1,0:T(8,128)} %moment_hbm.1, ...), custom_call_target="tpu_custom_call" | custom-call | tf_op jit(solution)/shard_map/pallas_call | solution.py:339
  33.5 1.1 %shard_map.85 = (f32[144,128]{1,0:T(8,128)}, f32[144,128]{1,0:T(8,128)}, f32[144,128]{1,0:T(8,128)}, bf16[768,768]{1,0:T(8,128)(2,1)}) custom-call(f32[144,128]{1,0:T(8,128)S(1)} %get-tuple-element.8.master_ref, f32[144,128]{1,0:T(8,128)S(1)} %get-tuple-element.9.moment_ref, f32[144,128]{1,0:T(8,128)S(1)} %get-tuple-element.10.second_ref, ...), custom_call_target="tpu_custom_call" | custom-call | tf_op jit(solution)/shard_map/pallas_call | solution.py:366

commit v3 on v2

--- a/solution.py
+++ b/solution.py
@@ -82,8 +82,8 @@
         return (kx * nz + kz) * ny + ky
 
     xs, zs, ys = range(1, nx), range(1, nz), range(1, ny)
-    peers = [peer(kc=1)] + [peer(kx=k) for k in xs]
-    peers += [peer(ky=k) for k in ys] + [peer(kz=k) for k in zs]
+    plane = [(p, q) for p in reversed(range(nx)) for q in reversed(range(ny)) if p + q]
+    peers = [peer(kc=1)] + [peer(kx=p, ky=q) for p, q in plane] + [peer(kz=k) for k in zs]
 
     barrier = pltpu.get_barrier_semaphore()
     for target in peers:
@@ -111,13 +111,16 @@
             [part[pl.ds(top, rows), s * lane:(s + 1) * lane] for s in range(strips)], axis=0
         )
 
+    def at_once(kz):
+        return kz == nz - 1 and nz > 1
+
     def x_first(kz):
         return kz % 2 == 0
 
     first, second_step, third = [], [], []
     for kz in reversed(range(nz)):
         for ky, kx in itertools.product(reversed(range(ny)), reversed(range(nx))):
-            if (kx if x_first(kz) else ky) != 0:
+            if (kx if x_first(kz) else ky) != 0 or (at_once(kz) and kx + ky):
                 first.append((kx, kz, ky))
             elif (ky if x_first(kz) else kx) != 0:
                 second_step.append((kx, kz, ky))
@@ -141,21 +144,6 @@
             device_id=peer(kc=1), device_id_type=MESH,
         ).wait_recv()
 
-    loads[0].wait()
-    for kx in reversed(range(nx)):
-        loads[nx - kx].wait()
-        part[columns(kx), :] = lax.dot_general(
-            acts_in[kx], grads_in[...], (((0,), (0,)), ((), ())),
-            preferred_element_type=jnp.float32,
-        )
-        if kx == nx - 1:
-            pl.semaphore_wait(barrier, len(peers))
-        for k in first + second_step + third:
-            if k[0] == kx:
-                i = slot(*k)
-                pair_out[i] = mine(*k, 1).astype(jnp.bfloat16)
-                send(pair_out.at[i], pair_in.at[i], pair_send.at[i], pair_recv.at[i], peer(kc=1))
-
     def take(i):
         arrived(inn.at[i], link_send.at[i], link_recv.at[i])
         return inn[i].astype(jnp.float32)
@@ -165,7 +153,11 @@
         i = slot(*k)
         arrived(pair_in.at[i], pair_send.at[i], pair_recv.at[i])
         value = mine(*k, 0) + pair_in[i].astype(jnp.float32)
-        if x_first(kz):
+        if at_once(kz):
+            if kx == 0 and ky == 0:
+                for p, q in plane:
+                    value += take(slot(p, kz, q))
+        elif x_first(kz):
             if kx == 0:
                 for p in xs:
                     value += take(slot(p, kz, ky))
@@ -186,18 +178,47 @@
         out[i] = total(k).astype(jnp.bfloat16)
         send(out.at[i], inn.at[i], link_send.at[i], link_recv.at[i], target)
 
+    def first_step(k):
+        kx, kz, ky = k
+        if at_once(kz):
+            pass_on(k, peer(kx=kx, ky=ky))
+        else:
+            pass_on(k, peer(kx=kx) if x_first(kz) else peer(ky=ky))
+
+    loads[0].wait()
+    for kx in reversed(range(nx)):
+        loads[nx - kx].wait()
+        halves = 2 if kx == 0 else 1
+        for half in range(halves):
+            wide = pl.ds(half * (strips * lane // halves), strips * lane // halves)
+            part[columns(kx), wide] = lax.dot_general(
+                acts_in[kx], grads_in[:, wide], (((0,), (0,)), ((), ())),
+                preferred_element_type=jnp.float32,
+            )
+            if kx == 0 and half == 0:
+                for k in first:
+                    if k[0] != 0:
+                        first_step(k)
+        if kx == nx - 1:
+            pl.semaphore_wait(barrier, len(peers))
+        for k in first + second_step + third:
+            if k[0] == kx:
+                i = slot(*k)
+                pair_out[i] = mine(*k, 1).astype(jnp.bfloat16)
+                send(pair_out.at[i], pair_in.at[i], pair_send.at[i], pair_recv.at[i], peer(kc=1))
+
     for k in first:
+        if k[0] == 0:
+            first_step(k)
+    gradient = None
+    for k in second_step + third:
         kx, kz, ky = k
-        pass_on(k, peer(kx=kx) if x_first(kz) else peer(ky=ky))
-    for k in second_step:
-        kx, kz, ky = k
-        pass_on(k, peer(ky=ky) if x_first(kz) else peer(kx=kx))
-    gradient = None
-    for k in third:
-        if k[1] != 0:
-            pass_on(k, peer(kz=k[1]))
+        if k == (0, 0, 0):
+            gradient = total(k)
+        elif k in third:
+            pass_on(k, peer(kz=kz))
         else:
-            gradient = total(k)
+            pass_on(k, peer(ky=ky) if x_first(kz) else peer(kx=kx))
     for kz in zs:
         gradient += take(slot(0, kz, 0))
 
@@ -235,50 +256,21 @@
     def spread(k):
         kx, kz, ky = k
         if kx == 0 and ky == 0 and kz == 0:
-            for p in reversed(zs):
+            for p in zs:
                 forward(k, 0, p, 0)
-        if x_first(kz):
-            if kx == 0 and ky == 0:
-                for p in ys:
-                    forward(k, 0, kz, p)
-            if kx == 0:
-                for p in xs:
-                    forward(k, p, kz, ky)
-        else:
-            if kx == 0 and ky == 0:
-                for p in xs:
-                    forward(k, p, kz, 0)
-            if ky == 0:
-                for p in ys:
-                    forward(k, kx, kz, p)
+        if kx == 0 and ky == 0:
+            for p, q in plane:
+                forward(k, p, kz, q)
         twin(k)
 
-    def middle(kz):
-        if x_first(kz):
-            return [(0, kz, p) for p in ys]
-        return [(p, kz, 0) for p in xs]
-
-    def last(kz):
-        if x_first(kz):
-            return [(p, kz, q) for q in range(ny) for p in xs]
-        return [(p, kz, q) for p in range(nx) for q in ys]
-
-    order = [(0, 0, 0)] + middle(0)
-    for kz in zs:
-        order += [(0, kz, 0)] + (last(kz - 1) if kz == 1 else middle(kz - 1))
-    order += middle(nz - 1)
-    for kz in zs:
-        order += last(kz)
-    seen = []
+    order = [(0, kz, 0) for kz in range(nz)]
+    order += [(p, kz, q) for kz in range(nz) for p, q in reversed(plane)]
     for k in order:
-        if k in seen:
-            continue
-        seen.append(k)
         if k != (0, 0, 0):
             receive(k)
         spread(k)
 
-    for k in seen:
+    for k in order:
         i = slot(*k)
         arrived(full.at[owner(*k, 1)], twin_send.at[i], twin_recv.at[i])
 

time: 34.9 us -> 30.6 us (0.88)
  Pallas kernels: 34 us -> 29.8 us
    pallas_call x1, Pallas kernels: 32.9 us -> 28.7 us  [fused(): pl.pallas_call(functools.partial(kernel, nx, nz, ny), out_shape=(pltpu.VM...]
where the time goes in v3:
time: 30.6 us; the launch traced here: 30.5 us
  Pallas kernels  29.8 us (97%)
  between operations  0.64 us (2%)
    pallas_call x1, Pallas kernels, fused(): pl.pallas_call(functools.partial(kernel, nx, nz, ny), out_shape=(pltpu.VM...  28.7 us
    pallas_call x1, Pallas kernels, fused(): pl.pallas_call(finish, out_shape=(jax.ShapeDtypeStruct(block, jnp.float32...  1.14 us

profile of v3, /device:TPU:0, one launch (start us, length us, event | category | flops | bytes accessed | tf_op | source)
XLA Modules:
  0.0 30.5 jit_solution(255471161166113203)
XLA Ops:
  0.6 28.7 %shard_map.84 = (f32[144,128]{1,0:T(8,128)S(1)}, f32[144,128]{1,0:T(8,128)S(1)}, f32[144,128]{1,0:T(8,128)S(1)}, bf16[32,144,128]{2,1,0:T(8,128)(2,1)S(1)}) custom-call(bf16[1280,768]{1,0:T(8,128)(2,1)} %acts_ref.1, bf16[1280,768]{1,0:T(8,128)(2,1)} %grads_ref.1, f32[144,128]{1,0:T(8,128)} %master_hbm.1, f32[144,128]{1,0:T(8,128)} %moment_hbm.1, ...), custom_call_target="tpu_custom_call" | custom-call | tf_op jit(solution)/shard_map/pallas_call | solution.py:331
  29.3 1.1 %shard_map.85 = (f32[144,128]{1,0:T(8,128)}, f32[144,128]{1,0:T(8,128)}, f32[144,128]{1,0:T(8,128)}, bf16[768,768]{1,0:T(8,128)(2,1)}) custom-call(f32[144,128]{1,0:T(8,128)S(1)} %get-tuple-element.8.master_ref, f32[144,128]{1,0:T(8,128)S(1)} %get-tuple-element.9.moment_ref, f32[144,128]{1,0:T(8,128)S(1)} %get-tuple-element.10.second_ref, ...), custom_call_target="tpu_custom_call" | custom-call | tf_op jit(solution)/shard_map/pallas_call | solution.py:358

commit v4 on v3

--- a/solution.py
+++ b/solution.py
@@ -56,8 +56,8 @@
 def kernel(
     nx, nz, ny,
     acts_ref, grads_ref, master_hbm, moment_hbm, second_hbm,
-    master_out, moment_out, second_out, full,
-    acts_in, grads_in, master_ref, moment_ref, second_ref, part, pair_out, pair_in, out, inn,
+    master_out, moment_out, second_out, weights,
+    acts_in, grads_in, master_ref, moment_ref, second_ref, part, pair_out, pair_in, out, inn, full,
     load, pair_send, pair_recv, link_send, link_recv,
     gather_send, gather_recv, twin_send, twin_recv,
 ):
@@ -270,46 +270,32 @@
             receive(k)
         spread(k)
 
+    chip_rows = CORES * rows
     for k in order:
         i = slot(*k)
         arrived(full.at[owner(*k, 1)], twin_send.at[i], twin_recv.at[i])
+        pair = owner(*k, 0) // CORES
+        top = pl.ds(pl.multiple_of(pair * chip_rows, chip_rows), chip_rows)
+        low = full[pair * CORES].astype(jnp.float32)
+        high = full[pair * CORES + 1].astype(jnp.float32)
+        for s in range(strips):
+            span = slice(s * rows, (s + 1) * rows)
+            both = jnp.concatenate([low[span], high[span]], axis=0)
+            weights[top, s * lane:(s + 1) * lane] = both.astype(jnp.bfloat16)
 
     for copy in started:
         copy.wait_send()
 
 
-def finish(
-    master_ref, moment_ref, second_ref, full,
-    master_out, moment_out, second_out, weights_out,
-    weights, store,
-):
-    blocks, _, lane = full.shape
-    rows = weights.shape[0] // blocks
-    strips = weights.shape[1] // lane
-    pairs = blocks // CORES
-    copies = []
-    plain = ((master_ref, master_out), (moment_ref, moment_out), (second_ref, second_out))
-    for i, (src, dst) in enumerate(plain):
-        copies.append(pltpu.make_async_copy(src, dst, store.at[i]))
-        copies[-1].start()
-    groups = 4 if pairs % 4 == 0 else 1
-    chip_rows = CORES * rows
-    for group in range(groups):
-        for pair in range(group * pairs // groups, (group + 1) * pairs // groups):
-            low = full[pair * CORES].astype(jnp.float32)
-            high = full[pair * CORES + 1].astype(jnp.float32)
-            for s in range(strips):
-                both = jnp.concatenate(
-                    [low[s * rows:(s + 1) * rows], high[s * rows:(s + 1) * rows]], axis=0
-                )
-                weights[pair * chip_rows:(pair + 1) * chip_rows, s * lane:(s + 1) * lane] = (
-                    both.astype(jnp.bfloat16)
-                )
-        span = pl.ds(group * (weights.shape[0] // groups), weights.shape[0] // groups)
-        copies.append(
-            pltpu.make_async_copy(weights.at[span, :], weights_out.at[span, :], store.at[3 + group])
-        )
-        copies[-1].start()
+def finish(*refs):
+    store = refs[-1]
+    half = (len(refs) - 1) // 2
+    copies = [
+        pltpu.make_async_copy(src, dst, store.at[i])
+        for i, (src, dst) in enumerate(zip(refs[:half], refs[half:-1]))
+    ]
+    for copy in reversed(copies):
+        copy.start()
     for copy in copies:
         copy.wait()
 
@@ -334,7 +320,7 @@
             pltpu.VMEM(block, jnp.float32),
             pltpu.VMEM(block, jnp.float32),
             pltpu.VMEM(block, jnp.float32),
-            pltpu.VMEM((chips * CORES,) + block, jnp.bfloat16),
+            pltpu.VMEM((width_in, width_out), jnp.bfloat16),
         ),
         in_specs=[pl.BlockSpec(memory_space=pltpu.HBM)] * 5,
         out_specs=(vmem,) * 4,
@@ -349,7 +335,8 @@
             pltpu.VMEM((chips,) + block, jnp.bfloat16),
             pltpu.VMEM((chips,) + block, jnp.bfloat16),
             pltpu.VMEM((chips,) + block, jnp.bfloat16),
-            pltpu.SemaphoreType.DMA((nx + 4,)),
+            pltpu.VMEM((chips * CORES,) + block, jnp.bfloat16),
+            pltpu.SemaphoreType.DMA((nx + 5,)),
         ] + [sems] * 8,
         compiler_params=pltpu.CompilerParams(
             collective_id=0, has_side_effects=True, vmem_limit_bytes=limit
@@ -366,8 +353,7 @@
         in_specs=[vmem] * 4,
         out_specs=(hbm,) * 4,
         scratch_shapes=[
-            pltpu.VMEM((width_in, width_out), jnp.bfloat16),
-            pltpu.SemaphoreType.DMA((7,)),
+            pltpu.SemaphoreType.DMA((4,)),
         ],
         compiler_params=pltpu.CompilerParams(vmem_limit_bytes=LIMIT),
     )(*results)

time: 30.6 us -> 30.6 us (level)
  no operation moved by 1% of the time
where the time goes in v4:
time: 30.6 us; the launch traced here: 30.5 us
  Pallas kernels  29.8 us (97%)
  between operations  0.64 us (2%)
    pallas_call x1, Pallas kernels, fused(): pl.pallas_call(functools.partial(kernel, nx, nz, ny), out_shape=(pltpu.VM...  28.7 us
    pallas_call x1, Pallas kernels, fused(): pl.pallas_call(finish, out_shape=(jax.ShapeDtypeStruct(block, jnp.float32...  1.11 us

profile of v4, /device:TPU:0, one launch (start us, length us, event | category | flops | bytes accessed | tf_op | source)
XLA Modules:
  0.0 30.5 jit_solution(1403779795215948485)
XLA Ops:
  0.6 28.7 %shard_map.84 = (f32[144,128]{1,0:T(8,128)S(1)}, f32[144,128]{1,0:T(8,128)S(1)}, f32[144,128]{1,0:T(8,128)S(1)}, bf16[768,768]{1,0:T(8,128)(2,1)S(1)}) custom-call(bf16[1280,768]{1,0:T(8,128)(2,1)} %acts_ref.1, bf16[1280,768]{1,0:T(8,128)(2,1)} %grads_ref.1, f32[144,128]{1,0:T(8,128)} %master_hbm.1, f32[144,128]{1,0:T(8,128)} %moment_hbm.1, ...), custom_call_target="tpu_custom_call" | custom-call | tf_op jit(solution)/shard_map/pallas_call | solution.py:317
  29.3 1.1 %shard_map.85 = (f32[144,128]{1,0:T(8,128)}, f32[144,128]{1,0:T(8,128)}, f32[144,128]{1,0:T(8,128)}, bf16[768,768]{1,0:T(8,128)(2,1)}) custom-call(f32[144,128]{1,0:T(8,128)S(1)} %get-tuple-element.8.refs_0_, f32[144,128]{1,0:T(8,128)S(1)} %get-tuple-element.9.refs_1_, f32[144,128]{1,0:T(8,128)S(1)} %get-tuple-element.10.refs_2_, ...), custom_call_target="tpu_custom_call" | custom-call | tf_op jit(solution)/shard_map/pallas_call | solution.py:345
